TPU v7x, 32 devices: a whole 2x2x4 slice. The times are simulated.
32 devices in a mesh: groups: 2 (over x), space: 4 (over y, core), frame: 4 (over z).
Axes of the slice: x: 2, y: 2, z: 4, core: 2. Of those that a mesh axis runs over, the one named last changes fastest.
Arguments:
- tokens: bfloat16 [4, 64, 128, 512], P('frame', ('groups', 'space')), parts along dimension 1, may hold values from -6 to 6
- src_brick: int32 [3, 64], P(None, 'groups'), parts along dimension 1, may hold values from 0 to 31, as said below
- merge_num: int32 [3, 64], P(None, 'groups'), parts along dimension 1, may hold values from 1 to 4
- gain_attn: float32 [512], replicated, may hold values from 0.1 to 1.9
- w_query: bfloat16 [512, 512], replicated, may hold values from -4 to 4
- w_key: bfloat16 [512, 512], replicated, may hold values from -4 to 4
- w_value: bfloat16 [512, 512], replicated, may hold values from -0.25 to 0.25
- w_out: bfloat16 [512, 512], replicated, may hold values from -0.25 to 0.25
- gain_mlp: float32 [512], replicated, may hold values from 0.1 to 1.9
- w_in: bfloat16 [512, 2048], replicated, may hold values from -0.25 to 0.25
- w_back: bfloat16 [2048, 512], replicated, may hold values from -0.125 to 0.125
Outputs:
- output: bfloat16 [4, 64, 128, 512], P('frame', ('groups', 'space')), parts along dimension 1
There are 2 independent parts, one for each index of `groups`. A program takes and returns all parts, laid end to end along the dimension named above; an argument that names none is the same for every part. Nothing has to cross between parts.
Inputs may be any that keep to these rules, and one draw needn't show every extreme that they name: `src_brick`: group the bricks in aligned groups of 8. Over all frames, at most 7 entries pair a target brick of one group with a source brick of one group, and for every target group some source group is paired exactly 7 times.
All inputs are finite; a program needn't handle non-finite values.
Results may differ from a plain program's by a relative error of at most 0.0069.
Values may be sent and summed in bfloat16 or wider, within the bound.
A program may use at most 64 MiB of HBM per device.

v0:
```python
import jax
import jax.numpy as jnp
from jax import lax
from jax.sharding import PartitionSpec as P

D = 512
HD = 64


def rms_norm(values_in, gain):
    as_float = values_in.astype(jnp.float32)
    mean_sq = jnp.mean(as_float * as_float, axis=-1, keepdims=True)
    return (as_float * lax.rsqrt(mean_sq + 1e-06) * gain).astype(jnp.bfloat16)


def temporal_block(merged, gain_attn, w_query, w_key, w_value, w_out, gain_mlp, w_in, w_back):
    frames_all, rows_all = (merged.shape[0], merged.shape[1])
    heads = D // HD
    normed = rms_norm(merged, gain_attn)
    queries = jnp.dot(normed, w_query, preferred_element_type=jnp.float32).astype(jnp.bfloat16)
    keys_proj = jnp.dot(normed, w_key, preferred_element_type=jnp.float32).astype(jnp.bfloat16)
    values_proj = jnp.dot(normed, w_value, preferred_element_type=jnp.float32).astype(jnp.bfloat16)
    query_heads = queries.reshape(frames_all, rows_all, heads, HD)
    key_heads = keys_proj.reshape(frames_all, rows_all, heads, HD)
    value_heads = values_proj.reshape(frames_all, rows_all, heads, HD)
    scores = jnp.einsum(
        "fmhd,gmhd->fghm", query_heads, key_heads, preferred_element_type=jnp.float32
    ) * (1.0 / HD**0.5)
    later = jnp.arange(frames_all)[:, None] >= jnp.arange(frames_all)[None, :]
    scores = jnp.where(later[:, :, None, None], scores, -1e30)
    row_max = jnp.max(scores, axis=1, keepdims=True)
    weights_exp = jnp.exp(scores - row_max)
    probs = (weights_exp / jnp.sum(weights_exp, axis=1, keepdims=True)).astype(jnp.bfloat16)
    context = jnp.einsum("fghm,gmhd->fmhd", probs, value_heads, preferred_element_type=jnp.float32)
    context = context.astype(jnp.bfloat16).reshape(frames_all, rows_all, D)
    mid = (
        merged.astype(jnp.float32) + jnp.dot(context, w_out, preferred_element_type=jnp.float32)
    ).astype(jnp.bfloat16)
    normed2 = rms_norm(mid, gain_mlp)
    hidden = jax.nn.gelu(jnp.dot(normed2, w_in, preferred_element_type=jnp.float32)).astype(
        jnp.bfloat16
    )
    return (
        mid.astype(jnp.float32) + jnp.dot(hidden, w_back, preferred_element_type=jnp.float32)
    ).astype(jnp.bfloat16)


def plan_slots(owners_all, source_rows, self_index, space_count, slot_cap, flat_rows):
    onehot = (owners_all[:, :, None] == jnp.arange(space_count)[None, None, :]).astype(jnp.int32)
    slot_rank = jnp.sum((jnp.cumsum(onehot, axis=1) - onehot) * onehot, axis=2)
    matched = (owners_all == self_index)[:, :, None] & (
        slot_rank[:, :, None] == jnp.arange(slot_cap)[None, None, :]
    )
    row_index = jnp.sum(matched.astype(jnp.int32) * source_rows[:, :, None], axis=1)
    is_valid = jnp.any(matched, axis=1)
    picked = jnp.take(flat_rows, row_index, axis=0)
    outgoing = jnp.where(is_valid[:, :, None, None], picked, jnp.zeros_like(picked))
    my_owner = lax.dynamic_index_in_dim(owners_all, self_index, 0, keepdims=False)
    my_rank = lax.dynamic_index_in_dim(slot_rank, self_index, 0, keepdims=False)
    return (outgoing, my_owner, my_rank)


def local(
    tokens, src_brick, merge_num, gain_attn, w_query, w_key, w_value, w_out, gain_mlp, w_in, w_back
):
    bricks_dev = tokens.shape[1]
    space_count = lax.axis_size("space")
    self_index = lax.axis_index("space")
    frames_all = src_brick.shape[0] + 1
    slot_cap = max(2, (frames_all - 1) * bricks_dev // space_count + 1)
    weights_mine = (
        lax.dynamic_slice_in_dim(merge_num, self_index * bricks_dev, bricks_dev, 1).astype(
            jnp.float32
        )
        * 0.25
    )
    stacked = lax.all_to_all(tokens, "frame", split_axis=2, concat_axis=0, tiled=True)
    slice_rows = stacked.shape[2]
    request_total = (frames_all - 1) * bricks_dev
    owners_all = (src_brick // bricks_dev).reshape(frames_all - 1, space_count, bricks_dev)
    owners_all = jnp.transpose(owners_all, (1, 0, 2)).reshape(space_count, request_total)
    local_rows = (src_brick % bricks_dev).reshape(frames_all - 1, space_count, bricks_dev)
    local_rows = jnp.transpose(local_rows, (1, 0, 2)).reshape(space_count, request_total)
    source_rows = (jnp.arange(request_total, dtype=jnp.int32) // bricks_dev * bricks_dev)[
        None, :
    ] + local_rows
    flat_rows = stacked.reshape(frames_all * bricks_dev, slice_rows, D)
    outgoing, my_owner, my_rank = plan_slots(
        owners_all, source_rows, self_index, space_count, slot_cap, flat_rows
    )
    received = lax.all_to_all(outgoing, "space", split_axis=0, concat_axis=0, tiled=True)
    pieces = received[my_owner, my_rank].reshape(frames_all - 1, bricks_dev, slice_rows, D)
    merged_rest = (
        stacked[1:].astype(jnp.float32)
        + weights_mine[:, :, None, None] * pieces.astype(jnp.float32)
    ).astype(jnp.bfloat16)
    merged = jnp.concatenate([stacked[:1], merged_rest], axis=0)
    slice_rows = merged.shape[2]
    rows_view = merged.reshape(frames_all, bricks_dev * slice_rows, D)
    result = temporal_block(
        rows_view, gain_attn, w_query, w_key, w_value, w_out, gain_mlp, w_in, w_back
    )
    result = result.reshape(frames_all, bricks_dev, slice_rows, D)
    return lax.all_to_all(result, "frame", split_axis=0, concat_axis=2, tiled=True)


def solution(mesh):
    in_specs = (
        P("frame", ("groups", "space"), None, None),
        P(None, "groups"),
        P(None, "groups"),
        P(),
        P(),
        P(),
        P(),
        P(),
        P(),
        P(),
        P(),
    )
    out_specs = P("frame", ("groups", "space"), None, None)
    return jax.shard_map(local, mesh=mesh, in_specs=in_specs, out_specs=out_specs, check_vma=False)
```

profile of v0, /device:TPU:0, one launch (start us, length us, event | category | flops | bytes accessed | tf_op | source)
XLA Modules:
  0.0 147.2 jit_solution(5047067707029519933)
XLA Ops:
  0.0 2.9 %copy.64 = bf16[1,8,128,512]{3,1,0,2:T(8,128)(2,1)} copy(bf16[1,8,128,512]{3,2,1,0:T(8,128)(2,1)} %param.11) | data formatting | bytes 2097152 | tf_op args[0]
  2.9 6.3 %all-to-all-start = ((bf16[1,8,128,512]{3,1,0,2:T(8,128)(2,1)}), bf16[1,8,128,512]{3,1,0,2:T(8,128)(2,1)S(1)}, u32[]{:S(2)}, u32[]{:S(2)}) async-start(bf16[1,8,128,512]{3,1,0,2:T(8,128)(2,1)} %copy.64), calls=%async_computation | async-start | bytes 2097152 | tf_op jit(solution)/shard_map/all_to_all | solution.py:77
  10.9 24.1 %all-to-all-done = bf16[1,8,128,512]{3,1,0,2:T(8,128)(2,1)S(1)} async-done(((bf16[1,8,128,512]{3,1,0,2:T(8,128)(2,1)}), bf16[1,8,128,512]{3,1,0,2:T(8,128)(2,1)S(1)}, u32[]{:S(2)}, u32[]{:S(2)}) %all-to-all-start) | async-done | bytes 1048608 | tf_op jit(solution)/shard_map/all_to_all | solution.py:77
  35.0 1.0 copy-done.1
  36.0 1.5 %copy.85 = bf16[1,8,4,32,512]{4,3,1,2,0:T(8,128)(2,1)S(1)} copy(bf16[1,8,4,32,512]{4,1,3,2,0:T(8,128)(2,1)} %bitcast.88) | data formatting | bytes 2097152 | tf_op jit(solution)/shard_map/all_to_all | solution.py:77
  37.5 1.5 %gather_fusion = bf16[28,32,512]{2,1,0:T(8,128)(2,1)} fusion(bf16[32,32,512]{2,1,0:T(8,128)(2,1)S(1)} %bitcast.82, s32[1024]{0:T(1024)S(1)} %pad_clamp_fusion), kind=kCustom, calls=%fused_computation | custom fusion | bytes 1835120 | tf_op jit(solution)/shard_map/jit(_take)/gather | solution.py:56
  39.1 2.3 %select_select_fusion = bf16[4,7,32,512]{3,2,1,0:T(8,128)(2,1)} fusion(bf16[4,7,32,512]{3,2,1,0:T(8,128)(2,1)} %bitcast.90, pred[4,7]{1,0:T(4,128)(4,1)S(1)} %copy.69, pred[4,7]{1,0:T(4,128)(4,1)S(1)} %copy.67), kind=kLoop, calls=%fused_computation.39 | loop fusion | flops 917504 | bytes 1835064 | tf_op jit(solution)/shard_map/jit(_where)/select_n | solution.py:57
  41.4 4.2 %all-to-all-start.1 = ((bf16[4,7,32,512]{3,2,1,0:T(8,128)(2,1)}), bf16[4,7,32,512]{3,2,1,0:T(8,128)(2,1)}, u32[]{:S(2)}, u32[]{:S(2)}) async-start(bf16[4,7,32,512]{3,2,1,0:T(8,128)(2,1)} %select_select_fusion), calls=%async_computation.1 | async-start | bytes 1835008 | tf_op jit(solution)/shard_map/all_to_all | solution.py:91
  45.9 1.0 slice.15
  46.9 11.8 %all-to-all-done.1 = bf16[4,7,32,512]{3,2,1,0:T(8,128)(2,1)} async-done(((bf16[4,7,32,512]{3,2,1,0:T(8,128)(2,1)}), bf16[4,7,32,512]{3,2,1,0:T(8,128)(2,1)}, u32[]{:S(2)}, u32[]{:S(2)}) %all-to-all-start.1) | async-done | bytes 917536 | tf_op jit(solution)/shard_map/all_to_all | solution.py:91
  58.7 2.8 %gather_fusion.1 = bf16[24,32,512]{2,1,0:T(8,128)(2,1)} fusion(bf16[4,7,32,512]{3,2,1,0:T(8,128)(2,1)} %all-to-all-done.1, s32[24]{0:T(128)S(1)} %or_bitcast_fusion), kind=kCustom, calls=%fused_computation.1 | custom fusion | bytes 1573056 | tf_op jit(solution)/shard_map/gather | solution.py:92
  61.5 1.5 %fusion.24 = bf16[3,256,512]{2,1,0:T(8,128)(2,1)S(1)} fusion(bf16[3,256,512]{2,1,0:T(8,128)(2,1)S(1)} %bitcast.91, f32[3,256]{1,0:T(4,128)S(1)} %mul.108, bf16[3,256,512]{2,1,0:T(8,128)(2,1)} %bitcast.92), kind=kLoop, calls=%fused_computation.32 | loop fusion | flops 1966080 | bytes 2362368 | tf_op jit(solution)/shard_map/convert_element_type | solution.py:96
  63.0 0.3 fusion.10
  63.3 0.6 copy-done.3
  63.9 1.7 %convolution_convert_fusion = bf16[4,256,512]{2,1,0:T(8,128)(2,1)} fusion(f32[512]{0:T(512)S(1)} %copy-done.9, f32[4,256]{1,0:T(4,128)S(1)} %add_rsqrt_fusion.1, bf16[512,512]{1,0:T(8,128)(2,1)S(1)} %copy-done.8, bf16[3,256,512]{2,1,0:T(8,128)(2,1)S(1)} %fusion.24, bf16[1,256,512]{2,1,0:T(8,128)(2,1)S(1)} %bitcast.96), kind=kOutput, calls=%fused_computation.33 | convolution fusion | flops 540016640 | bytes 2627584 | tf_op jit(solution)/shard_map/dot_general | solution.py:20
  65.6 1.5 %copy.73 = bf16[4,256,512]{1,2,0:T(8,128)(2,1)S(1)} copy(bf16[4,256,512]{2,1,0:T(8,128)(2,1)} %convolution_convert_fusion) | data formatting | bytes 2097152 | tf_op jit(solution)/shard_map/convert_element_type | solution.py:20
  67.1 2.5 %copy.75 = bf16[4,256,8,64]{3,0,1,2:T(4,128)(2,1)} copy(bf16[4,256,8,64]{1,3,2,0:T(8,128)(2,1)S(1)} %bitcast.85) | data formatting | bytes 2097152 | tf_op jit(solution)/shard_map/reshape | solution.py:23
  69.6 3.0 %convolution_convert_fusion.1 = bf16[4,256,512]{2,1,0:T(8,128)(2,1)} fusion(f32[512]{0:T(512)S(1)} %copy-done.9, f32[4,256]{1,0:T(4,128)S(1)} %add_rsqrt_fusion.1, bf16[512,512]{1,0:T(8,128)(2,1)} %param.16, bf16[3,256,512]{2,1,0:T(8,128)(2,1)} %copy-done.3, bf16[1,256,512]{2,1,0:T(8,128)(2,1)S(1)} %bitcast.97), kind=kOutput, calls=%fused_computation.34 | convolution fusion | flops 540016640 | bytes 2627584 | tf_op jit(solution)/shard_map/dot_general | solution.py:21
  72.6 1.5 %copy.72 = bf16[4,256,512]{1,2,0:T(8,128)(2,1)S(1)} copy(bf16[4,256,512]{2,1,0:T(8,128)(2,1)} %convolution_convert_fusion.1) | data formatting | bytes 2097152 | tf_op jit(solution)/shard_map/convert_element_type | solution.py:21
  74.1 2.5 %copy.74 = bf16[4,256,8,64]{3,0,1,2:T(4,128)(2,1)} copy(bf16[4,256,8,64]{1,3,2,0:T(8,128)(2,1)S(1)} %bitcast.86) | data formatting | bytes 2097152 | tf_op jit(solution)/shard_map/reshape | solution.py:24
  76.6 6.5 %fusion.58 = f32[8,256,4,4]{3,2,1,0:T(4,128)} fusion(bf16[4,256,8,64]{3,0,1,2:T(4,128)(2,1)} %copy.74, bf16[4,256,8,64]{3,0,1,2:T(4,128)(2,1)} %copy.75), kind=kOutput, calls=%fused_computation.92 | convolution fusion | flops 4194304 | bytes 2228224 | tf_op jit(solution)/shard_map/fmhd,gmhd->fghm/dot_general | solution.py:26
  83.0 2.8 %copy.76 = f32[8,256,4,4]{1,0,2,3:T(8,128)S(1)} copy(f32[8,256,4,4]{3,2,1,0:T(4,128)} %fusion.58) | data formatting | bytes 262144 | tf_op jit(solution)/shard_map/fmhd,gmhd->fghm/dot_general | solution.py:26
  86.2 4.3 %copy.78 = bf16[4,4,8,256]{1,0,2,3:T(4,128)(2,1)} copy(bf16[4,4,8,256]{3,2,1,0:T(8,128)(2,1)S(1)} %divide_convert_fusion) | data formatting | bytes 131072 | tf_op jit(solution)/shard_map/convert_element_type | solution.py:33
  90.5 2.8 %convolution_convert_fusion.2 = bf16[4,256,512]{2,1,0:T(8,128)(2,1)} fusion(f32[512]{0:T(512)S(1)} %copy-done.9, f32[4,256]{1,0:T(4,128)S(1)} %add_rsqrt_fusion.1, bf16[512,512]{1,0:T(8,128)(2,1)} %param.17, bf16[3,256,512]{2,1,0:T(8,128)(2,1)S(1)} %copy-done.4, bf16[1,256,512]{2,1,0:T(8,128)(2,1)S(1)} %bitcast.98), kind=kOutput, calls=%fused_computation.35 | convolution fusion | flops 540016640 | bytes 2627584 | tf_op jit(solution)/shard_map/dot_general | solution.py:22
  93.2 1.5 %copy.71 = bf16[4,256,512]{1,2,0:T(8,128)(2,1)S(1)} copy(bf16[4,256,512]{2,1,0:T(8,128)(2,1)} %convolution_convert_fusion.2) | data formatting | bytes 2097152 | tf_op jit(solution)/shard_map/convert_element_type | solution.py:22
  94.7 3.0 %copy.77 = bf16[4,256,8,64]{3,0,2,1:T(4,128)(2,1)} copy(bf16[4,256,8,64]{1,3,2,0:T(8,128)(2,1)S(1)} %bitcast.87) | data formatting | bytes 2097152 | tf_op jit(solution)/shard_map/reshape | solution.py:25
  97.7 5.9 %convert_bitcast_fusion = bf16[4,256,8,64]{3,0,2,1:T(4,128)(2,1)} fusion(bf16[4,256,8,64]{3,0,2,1:T(4,128)(2,1)} %copy.77, bf16[4,4,8,256]{1,0,2,3:T(4,128)(2,1)} %copy.78), kind=kOutput, calls=%fused_computation.29 | convolution fusion | flops 4718592 | bytes 2162688 | tf_op jit(solution)/shard_map/fghm,gmhd->fmhd/dot_general | solution.py:34
  103.6 4.2 %copy.79 = bf16[4,256,8,64]{1,3,2,0:T(8,128)(2,1)} copy(bf16[4,256,8,64]{3,0,2,1:T(4,128)(2,1)} %convert_bitcast_fusion) | data formatting | bytes 2097152 | tf_op jit(solution)/shard_map/convert_element_type | solution.py:35
  107.8 3.1 %fusion.14 = (f32[4,256]{1,0:T(4,128)S(1)}, bf16[4,256,512]{2,1,0:T(8,128)(2,1)}) fusion(bf16[4,256,512]{1,2,0:T(8,128)(2,1)} %bitcast.93, bf16[512,512]{1,0:T(8,128)(2,1)} %param.18, bf16[3,256,512]{2,1,0:T(8,128)(2,1)S(1)} %copy-done.5, bf16[1,256,512]{2,1,0:T(8,128)(2,1)S(1)} %bitcast.99), kind=kOutput, calls=%fused_computation.22 | convolution fusion | flops 540539904 | bytes 3674112 | tf_op jit(solution)/shard_map/dot_general | solution.py:37
  110.9 7.1 %fusion.17 = bf16[4,256,512]{2,1,0:T(8,128)(2,1)S(1)} fusion(bf16[4,256,512]{2,1,0:T(8,128)(2,1)} %get-tuple-element.10, bf16[2048,512]{1,0:T(8,128)(2,1)S(1)} %copy-done, bf16[512,2048]{1,0:T(8,128)(2,1)} %param.20, f32[512]{0:T(512)S(1)} %copy-done.10, f32[4,256]{1,0:T(4,128)S(1)} %add_rsqrt_fusion), kind=kOutput, calls=%fused_computation.25 | convolution fusion | flops 4317511680 | bytes 6297600 | tf_op jit(solution)/shard_map/dot_general | solution.py:44
  118.1 28.1 %all_to_all.38 = bf16[4,8,32,512]{3,2,1,0:T(8,128)(2,1)S(1)} all-to-all(bf16[4,8,32,512]{3,2,1,0:T(8,128)(2,1)S(1)} %bitcast.94), channel_id=1, replica_groups=mesh['groups'=2,'space'=4,'frame'=4] {'frame'}, dimensions={0} | all-to-all | bytes 2097152 | tf_op jit(solution)/shard_map/all_to_all | solution.py:104
  146.2 1.0 copy.81
  (53 shorter events, 2.2 us)
Async XLA Ops:
  0.0 110.9 %copy-start = (bf16[2048,512]{1,0:T(8,128)(2,1)S(1)}, bf16[2048,512]{1,0:T(8,128)(2,1)}, u32[]{:S(2)}) copy-start(bf16[2048,512]{1,0:T(8,128)(2,1)} %param.21) | copy-start | bytes 6291460
  0.0 9.3 %copy-start.6 = (s32[3,32]{1,0:T(4,128)S(1)}, s32[3,32]{1,0:T(4,128)}, u32[]{:S(2)}) copy-start(s32[3,32]{1,0:T(4,128)} %param.12) | copy-start | bytes 1156
  2.9 32.1 %all-to-all-start = ((bf16[1,8,128,512]{3,1,0,2:T(8,128)(2,1)}), bf16[1,8,128,512]{3,1,0,2:T(8,128)(2,1)S(1)}, u32[]{:S(2)}, u32[]{:S(2)}) async-start(bf16[1,8,128,512]{3,1,0,2:T(8,128)(2,1)} %copy.64), calls=%async_computation | async-start | bytes 2097152 | tf_op jit(solution)/shard_map/all_to_all | solution.py:77
  35.0 1.0 copy-start.1
  39.1 6.5 %copy-start.7 = (s32[3,32]{1,0:T(4,128)S(1)}, s32[3,32]{1,0:T(4,128)}, u32[]{:S(2)}) copy-start(s32[3,32]{1,0:T(4,128)} %param.13) | copy-start | bytes 1156
  41.4 17.3 %all-to-all-start.1 = ((bf16[4,7,32,512]{3,2,1,0:T(8,128)(2,1)}), bf16[4,7,32,512]{3,2,1,0:T(8,128)(2,1)}, u32[]{:S(2)}, u32[]{:S(2)}) async-start(bf16[4,7,32,512]{3,2,1,0:T(8,128)(2,1)} %select_select_fusion), calls=%async_computation.1 | async-start | bytes 1835008 | tf_op jit(solution)/shard_map/all_to_all | solution.py:91
  46.9 14.6 %copy-start.2 = (bf16[3,1,8,32,512]{4,3,2,0,1:T(8,128)(2,1)S(1)}, bf16[3,1,8,32,512]{4,3,2,0,1:T(8,128)(2,1)}, u32[]{:S(2)}) copy-start(bf16[3,1,8,32,512]{4,3,2,0,1:T(8,128)(2,1)} %slice.15) | copy-start | bytes 2359300
  61.5 2.4 %copy-start.8 = (bf16[512,512]{1,0:T(8,128)(2,1)S(1)}, bf16[512,512]{1,0:T(8,128)(2,1)}, u32[]{:S(2)}) copy-start(bf16[512,512]{1,0:T(8,128)(2,1)} %param.15) | copy-start | bytes 1572868
  61.5 2.4 %copy-start.9 = (f32[512]{0:T(512)S(1)}, f32[512]{0:T(512)}, u32[]{:S(2)}) copy-start(f32[512]{0:T(512)} %param.14) | copy-start | bytes 6148
  63.0 0.9 copy-start.3
  85.9 4.6 %copy-start.4 = (bf16[3,256,512]{2,1,0:T(8,128)(2,1)S(1)}, bf16[3,256,512]{2,1,0:T(8,128)(2,1)}, u32[]{:S(2)}) copy-start(bf16[3,256,512]{2,1,0:T(8,128)(2,1)} %copy-done.3) | copy-start | bytes 2359300
  103.6 4.2 %copy-start.5 = (bf16[3,256,512]{2,1,0:T(8,128)(2,1)S(1)}, bf16[3,256,512]{2,1,0:T(8,128)(2,1)}, u32[]{:S(2)}) copy-start(bf16[3,256,512]{2,1,0:T(8,128)(2,1)} %copy-done.3) | copy-start | bytes 2359300
  107.8 3.2 %copy-start.10 = (f32[512]{0:T(512)S(1)}, f32[512]{0:T(512)}, u32[]{:S(2)}) copy-start(f32[512]{0:T(512)} %param.19) | copy-start | bytes 6148
where the time goes:
time: 148 us; the launch traced here: 147 us
  local copies, waits for them, and re-layouts  37 us (25%)
  waiting for transfers between devices  35.9 us (24%)
  matrix products  30.1 us (20%)
  blocking collectives  28.1 us (19%)
  starting transfers between devices  10.6 us (7%)
  other arithmetic  5.3 us (4%)
    all_to_all x1, blocking collectives, local(): lax.all_to_all(result, 'frame', split_axis=0, concat_axis=2, tiled=True)  28.1 us
    all_to_all x1, waiting for transfers between devices, local(): lax.all_to_all(tokens, 'frame', split_axis=2, concat_axis=0, tiled=True)  24.1 us
    all_to_all x1, waiting for transfers between devices, local(): lax.all_to_all(outgoing, 'space', split_axis=0, concat_axis=0, tiled=True)  11.8 us
    dot_general x1, matrix products, temporal_block(): jnp.dot(hidden, w_back, preferred_element_type=jnp.float32)  7.12 us
    dot_general x1, matrix products, temporal_block(): jnp.einsum('fmhd,gmhd->fghm', query_heads, key_heads, preferred_element_t...  6.46 us
    all_to_all x1, starting transfers between devices, local(): lax.all_to_all(tokens, 'frame', split_axis=2, concat_axis=0, tiled=True)  6.35 us
    dot_general x1, matrix products, temporal_block(): jnp.einsum('fghm,gmhd->fmhd', probs, value_heads, preferred_element_type=...  5.87 us
    unnamed x23, local copies, waits for them, and re-layouts  4.57 us
  transfers between devices with their start and end apart: 2, of which 2 were waited for; matrix products, arithmetic and copies ran while one was open for 2% of the time, Pallas kernels for 0%

commit v1 on v0

v1 whole, which is shorter than its diff:
```python
import functools

import jax
import jax.numpy as jnp
from jax import lax
from jax.experimental import pallas as pl
from jax.experimental.pallas import tpu as pltpu
from jax.sharding import PartitionSpec as P

HD = 64
CHUNK = 16
MESH = pl.DeviceIdType.MESH
BF = jnp.bfloat16
F32 = jnp.float32


def norm_rows(values, gain):
    as_float = values.astype(F32)
    mean_sq = jnp.mean(as_float * as_float, axis=-1, keepdims=True)
    return (as_float * lax.rsqrt(mean_sq + 1e-06) * gain).astype(BF)


def matmul(left, right):
    return jnp.dot(left, right, preferred_element_type=F32)


def kernel(dims, *refs):
    n_f, n_s, nb, cr, nc, cap, d = dims
    rows_ref, pick_ref, weight_ref, tok, gain1, gain2 = refs[:6]
    weights_hbm = refs[6:12]
    out = refs[12]
    scratch = list(refs[13:])
    take = lambda count: [scratch.pop(0) for _ in range(count)]
    recv, pack, got, outb = take(nc), take(nc), take(nc), take(nc)
    wq, wk, wv, wo, wi, wb = weights_vmem = take(6)
    merged, nrm, q_s, k_s, v_s, acc = take(6)
    in_send, in_recv, y_send, y_recv, o_send, o_recv, own_in, own_out, wsem = take(9)
    rows = nb * cr
    ff = wi.shape[1]
    zi = lax.axis_index("frame")
    si = lax.axis_index("space")
    span = cr * nc
    f_order = sorted(range(1, n_f), key=lambda k: abs(k - n_f / 2))
    f_peers = [lax.rem(zi + k, n_f) for k in f_order]
    s_peers = [lax.rem(si + k, n_s) for k in range(1, n_s)]

    barrier = pltpu.get_barrier_semaphore()
    for z in f_peers:
        pl.semaphore_signal(barrier, inc=1, device_id={"frame": z}, device_id_type=MESH)
    for s in s_peers:
        pl.semaphore_signal(barrier, inc=1, device_id={"space": s}, device_id_type=MESH)
    pl.semaphore_wait(barrier, n_f - 1 + n_s - 1)

    def tok_at(z, c):
        start = pl.multiple_of(z * span + c * cr, cr)
        return tok.at[0, :, pl.ds(start, cr), :]

    def out_at(z, c):
        start = pl.multiple_of(z * span + c * cr, cr)
        return out.at[0, :, pl.ds(start, cr), :]

    def recv_at(c, f):
        return recv[c].at[pl.ds(f * nb, nb)]

    def in_copy(c, src, dst):
        return pltpu.make_async_remote_copy(
            src_ref=tok_at(dst, c), dst_ref=recv_at(c, src),
            send_sem=in_send.at[c, dst], recv_sem=in_recv.at[c, src],
            device_id={"frame": dst}, device_id_type=MESH)

    def own_in_copy(c):
        return pltpu.make_async_copy(tok_at(zi, c), recv_at(c, zi), own_in.at[c])

    def y_copy(c, src, dst):
        return pltpu.make_async_remote_copy(
            src_ref=pack[c].at[pl.ds(dst * cap, cap)], dst_ref=got[c].at[pl.ds(src * cap, cap)],
            send_sem=y_send.at[c, dst], recv_sem=y_recv.at[c, src],
            device_id={"space": dst}, device_id_type=MESH)

    def o_copy(c, src, dst):
        return pltpu.make_async_remote_copy(
            src_ref=outb[c].at[dst], dst_ref=out_at(src, c),
            send_sem=o_send.at[c, dst], recv_sem=o_recv.at[c, src],
            device_id={"frame": dst}, device_id_type=MESH)

    def own_out_copy(c):
        return pltpu.make_async_copy(outb[c].at[zi], out_at(zi, c), own_out.at[c])

    def weight_copy(i):
        return pltpu.make_async_copy(weights_hbm[i], weights_vmem[i], wsem.at[i])

    for c in range(nc):
        for z in f_peers:
            in_copy(c, zi, z).start()
        own_in_copy(c).start()
    for i in range(6):
        weight_copy(i).start()

    def exchange(c):
        for z in f_peers:
            in_copy(c, z, zi).wait_recv()
        own_in_copy(c).wait()

        def fill(dest, base):
            @pl.loop(0, cap)
            def _(j):
                dest[base + j] = recv[c][rows_ref[base + j]]

        for s in s_peers:
            fill(pack[c], s * cap)
            y_copy(c, si, s).start()
        fill(got[c], si * cap)

    def merge(c):
        for s in s_peers:
            y_copy(c, s, si).wait_recv()

        @pl.loop(0, nb)
        def _(b):
            merged[pl.ds(pl.multiple_of(b * cr, cr), cr), :] = recv[c][b]

        @pl.loop(0, (n_f - 1) * nb)
        def _(r):
            piece = got[c][pick_ref[r]].astype(F32) * weight_ref[r]
            total = recv[c][nb + r].astype(F32) + piece
            merged[pl.ds(pl.multiple_of((nb + r) * cr, cr), cr), :] = total.astype(BF)

    lane_a = lax.broadcasted_iota(jnp.int32, (4 * HD, 4 * HD), 0) // HD
    lane_b = lax.broadcasted_iota(jnp.int32, (4 * HD, 4 * HD), 1) // HD
    head_sum = jnp.where(lane_a == lane_b, 1.0 / HD**0.5, 0.0).astype(BF)

    def attend():
        nrm[...] = norm_rows(merged[...], gain1[...])
        q_s[...] = matmul(nrm[...], wq[...]).astype(BF)
        k_s[...] = matmul(nrm[...], wk[...]).astype(BF)
        v_s[...] = matmul(nrm[...], wv[...]).astype(BF)
        for f in range(n_f):
            here = slice(f * rows, (f + 1) * rows)
            for h in range(d // (4 * HD)):
                lanes = slice(h * 4 * HD, (h + 1) * 4 * HD)
                query = q_s[here, lanes].astype(F32)
                scores = []
                for g in range(f + 1):
                    prod = query * k_s[g * rows : (g + 1) * rows, lanes].astype(F32)
                    high = prod.astype(BF)
                    low = (prod - high.astype(F32)).astype(BF)
                    scores.append(matmul(high, head_sum) + matmul(low, head_sum))
                top = functools.reduce(jnp.maximum, scores)
                exps = [jnp.exp(s - top) for s in scores]
                inverse = 1.0 / functools.reduce(jnp.add, exps)
                total = 0.0
                for g in range(f + 1):
                    prob = (exps[g] * inverse).astype(BF).astype(F32)
                    total = total + prob * v_s[g * rows : (g + 1) * rows, lanes].astype(F32)
                nrm[here, lanes] = total.astype(BF)
        mid = (merged[...].astype(F32) + matmul(nrm[...], wo[...])).astype(BF)
        merged[...] = mid
        nrm[...] = norm_rows(mid, gain2[...])

    def feed(c):
        acc[...] = merged[...].astype(F32)

        @pl.loop(0, ff // d)
        def _(j):
            cols = pl.ds(pl.multiple_of(j * d, d), d)
            hidden = jax.nn.gelu(matmul(nrm[...], wi[:, cols])).astype(BF)
            acc[...] += matmul(hidden, wb[cols, :])

        outb[c][...] = acc[...].astype(BF).reshape(n_f, nb, cr, d)
        for z in f_peers:
            o_copy(c, zi, z).start()
        own_out_copy(c).start()

    exchange(0)
    for i in range(6):
        weight_copy(i).wait()
    for c in range(nc):
        merge(c)
        attend()
        if c + 1 < nc:
            exchange(c + 1)
        feed(c)

    for c in range(nc):
        for z in f_peers:
            in_copy(c, zi, z).wait_send()
            o_copy(c, zi, z).wait_send()
            o_copy(c, z, zi).wait_recv()
        own_out_copy(c).wait()
        for s in s_peers:
            y_copy(c, si, s).wait_send()


def slot_tables(src_brick, n_s, nb, cap, self_index):
    steps = src_brick.shape[0]
    request_total = steps * nb
    owners_all = (src_brick // nb).reshape(steps, n_s, nb)
    owners_all = jnp.transpose(owners_all, (1, 0, 2)).reshape(n_s, request_total)
    local_rows = (src_brick % nb).reshape(steps, n_s, nb)
    local_rows = jnp.transpose(local_rows, (1, 0, 2)).reshape(n_s, request_total)
    source_rows = (jnp.arange(request_total, dtype=jnp.int32) // nb * nb)[None, :] + local_rows
    earlier = jnp.arange(request_total)[:, None] > jnp.arange(request_total)[None, :]
    same = (owners_all[:, :, None] == owners_all[:, None, :]) & earlier[None]
    rank = jnp.sum(same.astype(jnp.int32), axis=2)
    matched = (owners_all == self_index)[:, :, None] & (
        rank[:, :, None] == jnp.arange(cap)[None, None, :]
    )
    row_index = jnp.sum(matched.astype(jnp.int32) * source_rows[:, :, None], axis=1)
    pick = lax.dynamic_index_in_dim(owners_all * cap + rank, self_index, 0, keepdims=False)
    return row_index.reshape(n_s * cap), pick


def local(
    tokens, src_brick, merge_num, gain_attn, w_query, w_key, w_value, w_out, gain_mlp, w_in, w_back
):
    nb, bt, d = tokens.shape[1:]
    ff = w_in.shape[1]
    n_s, n_f = lax.axis_size("space"), lax.axis_size("frame")
    self_index = lax.axis_index("space")
    cap = max(2, (n_f - 1) * nb // n_s + 1)
    span = bt // n_f
    cr = min(CHUNK, span)
    nc = span // cr
    mine = lax.dynamic_slice_in_dim(merge_num, self_index * nb, nb, 1)
    weights = (mine.astype(F32) * 0.25).reshape(-1)
    row_index, pick = slot_tables(src_brick, n_s, nb, cap, self_index)
    m = n_f * nb * cr
    smem = pl.BlockSpec(memory_space=pltpu.SMEM)
    vmem = pl.BlockSpec(memory_space=pltpu.VMEM)
    hbm = pl.BlockSpec(memory_space=pl.ANY)
    dma = pltpu.SemaphoreType.DMA
    scratch = (
        [pltpu.VMEM((n_f * nb, cr, d), BF) for _ in range(nc)]
        + [pltpu.VMEM((n_s * cap, cr, d), BF) for _ in range(2 * nc)]
        + [pltpu.VMEM((n_f, nb, cr, d), BF) for _ in range(nc)]
        + [pltpu.VMEM((d, d), BF)] * 4
        + [pltpu.VMEM((d, ff), BF), pltpu.VMEM((ff, d), BF)]
        + [pltpu.VMEM((m, d), BF)] * 5
        + [pltpu.VMEM((m, d), F32)]
        + [dma((nc, n_f)), dma((nc, n_f)), dma((nc, n_s)), dma((nc, n_s))]
        + [dma((nc, n_f)), dma((nc, n_f)), dma((nc,)), dma((nc,)), dma((6,))]
    )
    dims = (n_f, n_s, nb, cr, nc, cap, d)
    return pl.pallas_call(
        functools.partial(kernel, dims),
        out_shape=jax.ShapeDtypeStruct(tokens.shape, tokens.dtype),
        in_specs=[smem] * 3 + [hbm] + [vmem] * 2 + [hbm] * 6,
        out_specs=hbm,
        scratch_shapes=scratch,
        compiler_params=pltpu.CompilerParams(
            collective_id=0, has_side_effects=True, vmem_limit_bytes=56 << 20
        ),
        name="temporal_block",
    )(
        row_index, pick, weights, tokens, gain_attn.reshape(1, d), gain_mlp.reshape(1, d),
        w_query, w_key, w_value, w_out, w_in, w_back,
    )


def solution(mesh):
    tok_spec = P("frame", ("groups", "space"), None, None)
    in_specs = (tok_spec, P(None, "groups"), P(None, "groups")) + (P(),) * 8
    return jax.shard_map(
        local, mesh=mesh, in_specs=in_specs, out_specs=tok_spec, check_vma=False
    )
```

time: 148 us -> 62.2 us (0.42)
  the two profiles are of different devices: /device:TPU:0 before, /device:TPU:17 now
where the time goes in v1:
time: 62.2 us; the launch traced here: 62 us
  Pallas kernels  55.5 us (89%)
  local copies, waits for them, and re-layouts  4.5 us (7%)
  other arithmetic  1.91 us (3%)
    pallas_call x1, Pallas kernels, local(): pl.pallas_call(functools.partial(kernel, dims), out_shape=jax.ShapeDtypeS...  55.5 us
    unnamed x1, local copies, waits for them, and re-layouts  2.26 us

profile of v1, /device:TPU:17, one launch (start us, length us, event | category | flops | bytes accessed | tf_op | source)
XLA Modules:
  0.0 62.0 jit_solution(4450212351061643143)
XLA Ops:
  0.0 0.8 %convert_multiply_fusion = f32[3,8]{1,0:T(4,128)S(1)} fusion(s32[3,32]{1,0:T(4,128)} %param.13, s32[]{:T(128)S(6)} %select_n.32), kind=kLoop, calls=%fused_computation.10 | loop fusion | flops 48 | bytes 196 | tf_op jit(solution)/shard_map/mul | solution.py:225
  0.8 0.6 reshape.80.refs_2_
  1.4 0.7 %add_select_fusion.1 = (s32[3,32]{1,0:T(4,128)S(1)}, s32[3,32]{1,0:T(4,128)S(1)}) fusion(s32[3,32]{1,0:T(4,128)} %param.12), kind=kLoop, calls=%fused_computation.6 | loop fusion | flops 1824 | bytes 1152 | tf_op jit(solution)/shard_map/jit(floor_divide)/jit(_where)/select_n | solution.py:197
  2.1 0.1 reshape.75
  2.1 0.1 reshape.76
  2.2 0.2 convert_reduce_fusion
  2.5 0.6 dynamic-slice_bitcast_fusion.refs_1_
  3.1 0.1 reshape.77
  3.2 0.1 reshape.78
  3.3 0.2 select_reduce_fusion
  3.5 0.1 copy.18
  3.6 0.6 reshape.79.refs_0_
  4.2 55.5 %temporal_block.1 = bf16[1,8,128,512]{3,2,1,0:T(8,128)(2,1)} custom-call(s32[28]{0:T(128)} %reshape.79.refs_0_, s32[24]{0:T(128)} %dynamic-slice_bitcast_fusion.refs_1_, f32[24]{0:T(128)} %reshape.80.refs_2_, bf16[1,8,128,512]{3,2,1,0:T(8,128)(2,1)} %refs_3_.1, f32[1,512]{1,0:T(1,128)} %bitcast.8, f32[1,512]{1,0:T(1,128)} %bitcast.9, ...), custom_call_target="tpu_custom_call" | custom-call | tf_op jit(solution)/shard_map/temporal_block/pallas_call | solution.py:244
  59.7 2.3 %copy.20 = bf16[1,8,128,512]{3,2,1,0:T(8,128)(2,1)} copy(bf16[1,8,128,512]{3,2,1,0:T(8,128)(2,1)} %temporal_block.1) | data formatting | bytes 2097152
  (7 shorter events, 0.0 us)
